TPU v7x, 32 devices: a whole 2x2x4 slice. The times are simulated.
32 devices in a mesh: rep: 2 (over y), gx: 16 (over z, x, core).
Axes of the slice: x: 2, y: 2, z: 4, core: 2. Of those that a mesh axis runs over, the one named last changes fastest.
Arguments:
- positions: float32 [3, 49152], P(None, ('rep', 'gx')), parts along dimension 1, may hold values from 0 to 96
- velocities: float32 [3, 49152], P(None, ('rep', 'gx')), parts along dimension 1, may hold values from -9 to 9
- atom_params: float32 [4, 49152], P(None, ('rep', 'gx')), parts along dimension 1, may hold values from -1 to 2, as said below
- pair_list: int32 [3, 540672], P(None, ('rep', 'gx')), parts along dimension 1, may hold values from 0 to 479, as said below
- pair_count: int32 [32], P(('rep', 'gx')), parts along dimension 0, may hold values from 2112 to 16896, as said below
- exclusion: int32 [4, 540672], P(None, ('rep', 'gx')), parts along dimension 1, may hold values from 0 to 65535, as said below
- halo_far: int32 [3072], P(('rep', 'gx')), parts along dimension 0, may hold values from 0 to 191, as said below
- box_lengths: float32 [6], P('rep'), parts along dimension 0, may hold values from 12 to 96
- extended_variables: float32 [8], P('rep'), parts along dimension 0, may hold values from -0.3 to 0.3
Outputs:
- forces: float32 [3, 49152], P(None, ('rep', 'gx')), parts along dimension 1
- new_velocities: float32 [3, 49152], P(None, ('rep', 'gx')), parts along dimension 1
- new_positions: float32 [3, 49152], P(None, ('rep', 'gx')), parts along dimension 1
- new_coupling: float32 [8], P('rep'), parts along dimension 0
There are 2 independent parts, one for each index of `rep`. A program takes and returns all parts, laid end to end along the dimension named above; each array names one. Nothing has to cross between parts.
Inputs may be any that keep to these rules, and one draw needn't show every extreme that they name: `pair_list`: row 0 is a local cluster 0 to 191, row 1 a slot 0 to 479 of the slot table, row 2 an image code 0 to 8. Over each domain's used columns row 0 never falls (the list is grouped by its first cluster). Unused columns hold valid entries too. `pair_count`: at most 16896; some domain uses all 16896 columns in every draw. `exclusion`: each word holds 16 bits; bit 1 means the atom pair interacts. `halo_far`: 96 distinct local clusters of each domain. `atom_params`: rows 1 to 3 are positive.
All inputs are finite; a program needn't handle non-finite values.
Results may differ from a plain program's by a relative error of at most 0.0003.
Values sent between devices are 32-bit elements; how exact they have to be, the bound alone decides.
A program may use at most 64 MiB of HBM per device.

v0:
```python
import functools

import jax
import jax.numpy as jnp
from jax import lax
from jax.experimental import pallas as pl
from jax.experimental.pallas import tpu as pltpu
from jax.sharding import PartitionSpec as P

time_step = 0.25
reaction_term = 1.0 / 1331.0
thermal_scale_unit = 2.0
reservoir_inertia_mass = 4.0
barostat_gain = 0.1
pressure_target = 1.0

LANES = 128


def round_up(value, unit):
    return (value + unit - 1) // unit * unit


def split_three(value):
    high = value.astype(jnp.bfloat16).astype(jnp.float32)
    rest = value - high
    middle = rest.astype(jnp.bfloat16).astype(jnp.float32)
    return jnp.concatenate([high, middle, rest - middle], axis=0).astype(jnp.bfloat16)


def one_hot_rows(index_row, rows, ramp):
    pieces = []
    for base in range(0, rows, 256):
        height = min(256, rows - base)
        moved = (index_row - base).astype(jnp.float32)
        moved = jnp.broadcast_to(moved, (16, LANES)).astype(jnp.bfloat16)
        for first in range(0, height, 16):
            hit = moved == ramp[first : first + 16]
            pieces.append(jnp.where(hit, jnp.bfloat16(1), jnp.bfloat16(0)))
    return jnp.concatenate(pieces, axis=0)


def gathered(table_ref, index_row, tiles):
    index = jnp.broadcast_to(index_row, (8, LANES))
    within = index & (LANES - 1)
    block = index // LANES
    result = []
    for component in range(6):
        value = None
        for tile in range(tiles):
            source = table_ref[component * 8 : component * 8 + 8, tile * LANES : (tile + 1) * LANES]
            picked = jnp.take_along_axis(source, within, axis=1, mode="promise_in_bounds")
            value = picked if value is None else jnp.where(block == tile, picked, value)
        result.append(value)
    return result


def pair_kernel(
    count_ref, box_ref, lift_ref, here_ref, near_ref, beyond_ref, chosen_ref, velocity_ref,
    param_ref, pair_ref, word_ref, own_out, near_out, far_out, sum_ref,
    table_ref, wide_ref, virial_ref, first_got, second_got, bits_got, first_terms, second_terms,
    own_ref, other_ref, *, clusters, slots, block
):
    sublane = lax.broadcasted_iota(jnp.int32, (8, LANES), 0)
    lane = lax.broadcasted_iota(jnp.int32, (8, LANES), 1)
    ramp = lax.broadcasted_iota(jnp.int32, (256, LANES), 0).astype(jnp.float32).astype(jnp.bfloat16)
    count = count_ref[0]
    box_y = box_ref[1]
    box_z = box_ref[2]
    first_tiles = -(-clusters // LANES)
    second_tiles = -(-slots // LANES)
    near_lift = jnp.where(lift_ref[0] >= 1, box_ref[0], 0.0)
    far_lift = jnp.where(lift_ref[0] >= 0, box_ref[0], 0.0)
    upper = lax.broadcasted_iota(jnp.int32, (48, clusters), 0) < 8
    tail = slots - slots % LANES
    if tail < table_ref.shape[1]:
        table_ref[:, tail:] = jnp.zeros((48, table_ref.shape[1] - tail), jnp.float32)
    table_ref[:, 0:clusters] = here_ref[...]
    table_ref[:, clusters : 2 * clusters] = near_ref[...] + jnp.where(upper, near_lift, 0.0)
    wide_ref[...] = jnp.zeros_like(wide_ref)
    wide_ref[:, 0:clusters] = beyond_ref[...]
    far_count = slots - 2 * clusters
    for start in range(0, far_count, LANES):
        width = min(LANES, far_count - start)
        values = gathered(wide_ref, chosen_ref[0:1, start : start + LANES], first_tiles)
        values[0] = values[0] + far_lift
        for component in range(6):
            table_ref[
                component * 8 : component * 8 + 8, 2 * clusters + start : 2 * clusters + start + width
            ] = values[component][:, :width]
    own_ref[...] = jnp.zeros_like(own_ref)
    other_ref[...] = jnp.zeros_like(other_ref)
    virial_ref[...] = jnp.zeros_like(virial_ref)
    first_terms[...] = jnp.zeros_like(first_terms)
    second_terms[...] = jnp.zeros_like(second_terms)

    def fetch(number, part):
        at = pl.multiple_of(number * block + part * LANES, LANES)
        here = pl.ds(at, LANES)
        lanes = slice(part * LANES, (part + 1) * LANES)
        image = jnp.broadcast_to(pair_ref[2:3, here], (8, LANES))
        first = gathered(table_ref, pair_ref[0:1, here], first_tiles)
        second = gathered(table_ref, pair_ref[1:2, here], second_tiles)
        step_y = jnp.where(image >= 6, 1.0, jnp.where(image >= 3, 0.0, -1.0))
        step_z = image.astype(jnp.float32) - 3.0 * step_y - 4.0
        shift = (None, step_y * box_y, step_z * box_z)
        for c in range(3):
            origin = jnp.broadcast_to(first[c][0:1], (8, LANES))
            second[c] = second[c] - origin
            if shift[c] is not None:
                second[c] = second[c] + shift[c]
            first[c] = first[c] - origin
        words = [jnp.broadcast_to(word_ref[w : w + 1, here], (8, LANES)) for w in range(4)]
        low = jnp.where(sublane < 2, words[0], words[1])
        high = jnp.where(sublane < 6, words[2], words[3])
        bits = jnp.where(sublane < 4, low, high) >> (8 * (sublane & 1))
        bits_got[:, lanes] = jnp.where(at + lane < count, bits, 0)
        first[4] = 6.0 * first[4]
        first[5] = 12.0 * first[5]
        for c in range(6):
            first_got[c * 8 : c * 8 + 8, lanes] = first[c]
            second_got[c * 8 : c * 8 + 8, lanes] = second[c]

    def interact(part):
        lanes = slice(part * LANES, (part + 1) * LANES)
        first = [first_got[c * 8 : c * 8 + 8, lanes] for c in range(6)]
        second = [second_got[c * 8 : c * 8 + 8, lanes] for c in range(6)]
        bits = bits_got[:, lanes]
        charge, dispersion, repulsion = first[3], first[4], first[5]
        moving = second
        onto_first = [None] * 3
        onto_second = [None] * 3
        for turn in range(7, -1, -1):
            moving = [pltpu.roll(m, 1, 0) for m in moving] if turn else second
            delta = [moving[c] - first[c] for c in range(3)]
            radius_sq = delta[0] * delta[0] + delta[1] * delta[1] + delta[2] * delta[2]
            inverse = lax.rsqrt(radius_sq)
            inverse_sq = inverse * inverse
            cube = inverse * inverse_sq
            six = cube * cube
            scalar = charge * moving[3] * (cube - reaction_term) + (
                repulsion * moving[5] * six - dispersion * moving[4]
            ) * (six * inverse_sq)
            wanted = (bits & (1 << ((sublane + turn) & 7))) != 0
            scalar = jnp.where(wanted, scalar, 0.0)
            for c in range(3):
                force = scalar * delta[c]
                if onto_first[c] is None:
                    onto_first[c] = -force
                    onto_second[c] = force
                else:
                    onto_first[c] = onto_first[c] - force
                    onto_second[c] = pltpu.roll(onto_second[c], 1, 0) + force
        first_terms[:, lanes] = split_three(jnp.concatenate(onto_first, axis=0))
        second_terms[:, lanes] = split_three(jnp.concatenate(onto_second, axis=0))
        return [onto_second[c] * second[c] + onto_first[c] * first[c] for c in range(3)]

    def spread(number):
        first_hot = []
        second_hot = []
        for part in range(block // LANES):
            here = pl.ds(pl.multiple_of(number * block + part * LANES, LANES), LANES)
            first_hot.append(one_hot_rows(pair_ref[0:1, here], clusters, ramp))
            second_hot.append(one_hot_rows(pair_ref[1:2, here], slots, ramp))
        contract = (((1,), (1,)), ((), ()))
        own_ref[...] += lax.dot_general(
            first_terms[...], jnp.concatenate(first_hot, axis=1), contract,
            preferred_element_type=jnp.float32,
        )
        other_ref[...] += lax.dot_general(
            second_terms[...], jnp.concatenate(second_hot, axis=1), contract,
            preferred_element_type=jnp.float32,
        )

    blocks = jnp.maximum((count + block - 1) // block, 1)
    for part in range(block // LANES):
        fetch(0, part)

    def one_block(number, carry):
        spread(jnp.maximum(number - 1, 0))
        upcoming = jnp.minimum(number + 1, blocks - 1)
        virial = [virial_ref[c * 8 : c * 8 + 8, :] for c in range(3)]
        for part in range(block // LANES):
            added = interact(part)
            virial = [virial[c] + added[c] for c in range(3)]
            fetch(upcoming, part)
        for c in range(3):
            virial_ref[c * 8 : c * 8 + 8, :] = virial[c]
        return carry

    lax.fori_loop(0, blocks, one_block, 0)
    spread(blocks - 1)
    other = other_ref[0:24, :] + other_ref[24:48, :] + other_ref[48:72, :]
    own_out[...] = own_ref[0:24, :] + own_ref[24:48, :] + own_ref[48:72, :] + other[:, 0:clusters]
    near_out[...] = other[:, clusters : 2 * clusters]
    far_sum = jnp.zeros((72, clusters), jnp.float32)
    for start in range(0, far_count, LANES):
        width = min(LANES, far_count - start)
        piece = other[:, 2 * clusters + start : 2 * clusters + start + width]
        if width < LANES:
            piece = jnp.concatenate([piece, jnp.zeros((24, LANES - width), jnp.float32)], axis=1)
        far_sum = far_sum + lax.dot_general(
            split_three(piece),
            one_hot_rows(chosen_ref[0:1, start : start + LANES], clusters, ramp),
            (((1,), (1,)), ((), ())), preferred_element_type=jnp.float32,
        )
    far_out[...] = far_sum[0:24] + far_sum[24:48] + far_sum[48:72]
    energy = velocity_ref[...] * velocity_ref[...] / param_ref[3:4, :]
    energy = 0.5 * jnp.sum(energy, axis=1, keepdims=True)
    rows = [
        jnp.sum(jnp.sum(virial_ref[c * 8 : c * 8 + 8, :], axis=0, keepdims=True), axis=1, keepdims=True) * -0.5
        for c in range(3)
    ]
    rows = rows + [energy, jnp.zeros((2, 1), jnp.float32)]
    sum_ref[...] = jnp.broadcast_to(jnp.concatenate(rows, axis=0), (8, LANES))


def pair_forces(scalars, arrays, pair_list, exclusion, clusters, slots):
    pairs = pair_list.shape[1]
    block = next(b for b in (512, 384, 256, 128) if pairs % b == 0)
    vmem = pl.BlockSpec(memory_space=pltpu.VMEM)
    smem = pl.BlockSpec(memory_space=pltpu.SMEM)
    folded = jax.ShapeDtypeStruct((24, clusters), jnp.float32)
    return pl.pallas_call(
        functools.partial(pair_kernel, clusters=clusters, slots=slots, block=block),
        name="pair_kernel",
        out_shape=(folded, folded, folded, jax.ShapeDtypeStruct((8, LANES), jnp.float32)),
        in_specs=[smem] * 3 + [vmem] * 8,
        out_specs=(vmem,) * 4,
        scratch_shapes=[
            pltpu.VMEM((48, round_up(slots, LANES)), jnp.float32),
            pltpu.VMEM((48, round_up(clusters, LANES)), jnp.float32),
            pltpu.VMEM((24, LANES), jnp.float32),
            pltpu.VMEM((48, block), jnp.float32),
            pltpu.VMEM((48, block), jnp.float32),
            pltpu.VMEM((8, block), jnp.int32),
            pltpu.VMEM((72, block), jnp.bfloat16),
            pltpu.VMEM((72, block), jnp.bfloat16),
            pltpu.VMEM((72, clusters), jnp.float32),
            pltpu.VMEM((72, slots), jnp.float32),
        ],
    )(*scalars, *arrays, pair_list, exclusion)


def final_kernel(
    own_ref, near_ref, far_ref, rate_ref, position_ref, velocity_ref, param_ref,
    force_out, velocity_out, position_out, folded_ref, *, clusters
):
    sublane = lax.broadcasted_iota(jnp.int32, (8, LANES), 0)
    lane = lax.broadcasted_iota(jnp.int32, (8, LANES), 1)
    wanted = sublane == (lane & 7)
    folded_ref[...] = jnp.zeros_like(folded_ref)
    folded_ref[:, 0:clusters] = own_ref[...] + near_ref[...] + far_ref[...]
    for c in range(3):
        for tile in range(clusters * 8 // LANES):
            at = tile * 16
            source = folded_ref[c * 8 : c * 8 + 8, at // LANES * LANES : at // LANES * LANES + LANES]
            picked = jnp.take_along_axis(
                source, at % LANES + lane // 8, axis=1, mode="promise_in_bounds"
            )
            force_out[c : c + 1, tile * LANES : (tile + 1) * LANES] = jnp.sum(
                jnp.where(wanted, picked, 0.0), axis=0, keepdims=True
            )
    rates = rate_ref[0:3, 0:1]
    damping = rate_ref[3:4, 0:1]
    velocity = velocity_ref[...]
    moved = velocity + time_step * (
        force_out[...] * param_ref[3:4, :] - (damping + rates) * velocity
    )
    velocity_out[...] = moved
    position_out[...] = position_ref[...] * (1.0 + time_step * rates) + time_step * moved


def finished(own, near_back, far_back, rates, positions, velocities, atom_params):
    vmem = pl.BlockSpec(memory_space=pltpu.VMEM)
    clusters = own.shape[1]
    shape = jax.ShapeDtypeStruct(positions.shape, jnp.float32)
    return pl.pallas_call(
        functools.partial(final_kernel, clusters=clusters),
        name="final_kernel",
        out_shape=(shape,) * 3,
        in_specs=[vmem] * 7,
        out_specs=(vmem,) * 3,
        scratch_shapes=[pltpu.VMEM((24, round_up(clusters, LANES)), jnp.float32)],
    )(own, near_back, far_back, rates, positions, velocities, atom_params)


def send(source, target, sems, place, device):
    return pltpu.make_async_remote_copy(
        src_ref=source,
        dst_ref=target,
        send_sem=sems[0].at[place],
        recv_sem=sems[1].at[place],
        device_id={"gx": device},
        device_id_type=pl.DeviceIdType.MESH,
    )


def forward_kernel(packed_ref, chosen_ref, near_ref, beyond_ref, picked_ref, send_sems, recv_sems, *, count):
    me = lax.axis_index("gx")
    barrier = pltpu.get_barrier_semaphore()
    for step in (1, 2, count - 1, count - 2):
        pl.semaphore_signal(
            barrier, inc=1, device_id={"gx": lax.rem(me + step, count)},
            device_id_type=pl.DeviceIdType.MESH,
        )
    pl.semaphore_wait(barrier, 4)
    below = lax.rem(me + count - 1, count)
    far_below = lax.rem(me + count - 2, count)
    sems = (send_sems, recv_sems)
    copies = [
        send(packed_ref, beyond_ref, sems, 1, far_below),
        send(chosen_ref, picked_ref, sems, 2, far_below),
        send(packed_ref, near_ref, sems, 0, below),
    ]
    for copy in copies:
        copy.start()
    for copy in copies:
        copy.wait()


def forward(packed, chosen, count):
    vmem = pl.BlockSpec(memory_space=pltpu.VMEM)
    return pl.pallas_call(
        functools.partial(forward_kernel, count=count),
        name="forward_kernel",
        out_shape=(
            jax.ShapeDtypeStruct(packed.shape, packed.dtype),
            jax.ShapeDtypeStruct(packed.shape, packed.dtype),
            jax.ShapeDtypeStruct(chosen.shape, chosen.dtype),
        ),
        in_specs=[vmem] * 2,
        out_specs=(vmem,) * 3,
        scratch_shapes=[pltpu.SemaphoreType.DMA((3,)), pltpu.SemaphoreType.DMA((3,))],
        compiler_params=pltpu.CompilerParams(collective_id=0, has_side_effects=True),
    )(packed, chosen)


def return_kernel(
    box_ref, extended_ref, near_ref, far_ref, sum_ref, near_back, far_back, rate_ref,
    all_sums, send_sems, recv_sems, give_sems, take_sems, *, count, particles
):
    me = lax.axis_index("gx")
    barrier = pltpu.get_barrier_semaphore()

    def greet(step, carry):
        pl.semaphore_signal(
            barrier, inc=1, device_id={"gx": lax.rem(me + step, count)},
            device_id_type=pl.DeviceIdType.MESH,
        )
        return carry

    lax.fori_loop(1, count, greet, 0)
    pl.semaphore_wait(barrier, count - 1)
    sems = (send_sems, recv_sems)
    copies = [
        send(far_ref, far_back, sems, 1, lax.rem(me + 2, count)),
        send(near_ref, near_back, sems, 0, lax.rem(me + 1, count)),
    ]

    def sum_copy(step, source):
        return pltpu.make_async_remote_copy(
            src_ref=sum_ref,
            dst_ref=all_sums.at[source],
            send_sem=give_sems.at[step],
            recv_sem=take_sems.at[source],
            device_id={"gx": lax.rem(me + step, count)},
            device_id_type=pl.DeviceIdType.MESH,
        )

    def give(step, carry):
        sum_copy(step, me).start()
        return carry

    def take(step, carry):
        sum_copy(step, lax.rem(me + count - step, count)).wait()
        return carry

    lax.fori_loop(1, count, give, 0)
    for copy in copies:
        copy.start()
    all_sums[me] = sum_ref[...]
    lax.fori_loop(1, count, take, 0)
    total = lax.fori_loop(
        0, count, lambda source, held: held + all_sums[source], jnp.zeros((8, LANES), jnp.float32)
    )
    virial = total[0:3]
    kinetic = total[3:6]
    energy = total[3:4] + total[4:5] + total[5:6]
    volume = box_ref[0] * box_ref[1] * box_ref[2]
    ratio = 2.0 * energy / (3.0 * particles * thermal_scale_unit)
    rate_ref[3:4] = extended_ref[0] + reservoir_inertia_mass * (ratio - 1.0)
    change = barostat_gain * (kinetic - virial - pressure_target * volume / 2.0) / (energy / 3.0)
    for c in range(3):
        rate_ref[c : c + 1] = extended_ref[1 + c] + change[c : c + 1]
    for copy in copies:
        copy.wait()


def returned(box_lengths, extended_variables, near, far, sums, count, particles):
    vmem = pl.BlockSpec(memory_space=pltpu.VMEM)
    smem = pl.BlockSpec(memory_space=pltpu.SMEM)
    return pl.pallas_call(
        functools.partial(return_kernel, count=count, particles=particles),
        name="return_kernel",
        out_shape=(
            jax.ShapeDtypeStruct(near.shape, near.dtype),
            jax.ShapeDtypeStruct(far.shape, far.dtype),
            jax.ShapeDtypeStruct((4, LANES), jnp.float32),
        ),
        in_specs=[smem] * 2 + [vmem] * 3,
        out_specs=(vmem,) * 3,
        scratch_shapes=[
            pltpu.VMEM((count, 8, LANES), jnp.float32),
            pltpu.SemaphoreType.DMA((2,)),
            pltpu.SemaphoreType.DMA((2,)),
            pltpu.SemaphoreType.DMA((count,)),
            pltpu.SemaphoreType.DMA((count,)),
        ],
        compiler_params=pltpu.CompilerParams(collective_id=1, has_side_effects=True),
    )(box_lengths, extended_variables, near, far, sums)


def on_device(
    positions,
    velocities,
    atom_params,
    pair_list,
    pair_count,
    exclusion,
    halo_far,
    box_lengths,
    extended_variables,
):
    atoms_here = positions.shape[1]
    clusters = atoms_here // 8
    far_clusters = halo_far.shape[0]
    slots = 2 * clusters + far_clusters
    axis_count = lax.axis_size("gx")
    packed = jnp.concatenate([positions, atom_params[:3]], axis=0)
    packed = packed.reshape(6, clusters, 8).transpose(0, 2, 1).reshape(48, clusters)
    chosen = jnp.pad(halo_far, (0, round_up(far_clusters, LANES) - far_clusters))[None, :]
    near_rows, beyond, picked = forward(packed, chosen, axis_count)
    lift = (lax.axis_index("gx") - (axis_count - 2)).astype(jnp.int32)[None]
    own, near, far, sums = pair_forces(
        (pair_count, box_lengths, lift),
        (packed, near_rows, beyond, picked, velocities, atom_params),
        pair_list, exclusion, clusters, slots,
    )
    near_back, far_back, rates = returned(
        box_lengths, extended_variables, near, far, sums, axis_count, atoms_here * axis_count
    )
    forces, new_velocities, new_positions = finished(
        own, near_back, far_back, rates, positions, velocities, atom_params
    )
    new_coupling = jnp.concatenate([rates[3:, 0], rates[:3, 0]])
    return (forces, new_velocities, new_positions, new_coupling)


def solution(mesh):
    return jax.shard_map(
        on_device,
        mesh=mesh,
        in_specs=(
            P(None, ("rep", "gx")),
            P(None, ("rep", "gx")),
            P(None, ("rep", "gx")),
            P(None, ("rep", "gx")),
            P(("rep", "gx")),
            P(None, ("rep", "gx")),
            P(("rep", "gx")),
            P("rep"),
            P("rep"),
        ),
        out_specs=(
            P(None, ("rep", "gx")),
            P(None, ("rep", "gx")),
            P(None, ("rep", "gx")),
            P("rep"),
        ),
        check_vma=False,
    )
```

profile of v0, /device:TPU:0, one launch (start us, length us, event | category | flops | bytes accessed | tf_op | source)
XLA Modules:
  0.0 42.3 jit_solution(18320250944411534070)
XLA Ops:
  0.6 0.8 %pad_maximum_fusion = f32[6,1536]{1,0:T(8,128)S(1)} fusion(f32[3,1536]{1,0:T(4,128)} %bitcast.10, f32[3,1536]{1,0:T(4,128)} %position_ref.1), kind=kLoop, calls=%fused_computation | loop fusion | flops 9216 | bytes 73728 | tf_op jit(solution)/shard_map/concatenate | solution.py:440
  1.4 0.3 reshape.14
  1.7 0.9 %copy.14 = f32[6,8,192]{2,1,0:T(8,128)} copy(f32[6,8,192]{1,2,0:T(8,128)S(1)} %bitcast.7) | data formatting | bytes 73728 | tf_op jit(solution)/shard_map/transpose | solution.py:441
  2.6 0.0 copy-start.1
  2.6 0.7 %copy-done.1 = s32[96]{0:T(128)S(1)} copy-done((s32[96]{0:T(128)S(1)}, s32[96]{0:T(128)}, u32[]{:S(2)}) %copy-start.1) | copy-done | bytes 408
  3.3 0.5 %pad_bitcast_fusion.chosen_ref = s32[1,128]{1,0:T(1,128)} fusion(s32[96]{0:T(128)S(1)} %copy-done.1), kind=kLoop, calls=%fused_computation.3 | loop fusion | bytes 896 | tf_op jit(solution)/shard_map/broadcast_in_dim | solution.py:442
  3.8 9.7 %forward_kernel.1 = (f32[48,192]{1,0:T(8,128)}, f32[48,192]{1,0:T(8,128)}, s32[1,128]{1,0:T(1,128)}) custom-call(f32[48,192]{1,0:T(8,128)} %bitcast.8, s32[1,128]{1,0:T(1,128)} %pad_bitcast_fusion.chosen_ref), custom_call_target="tpu_custom_call" | custom-call | tf_op jit(solution)/shard_map/forward_kernel/pallas_call | solution.py:324
  14.1 7.4 %pair_kernel.1 = (f32[24,192]{1,0:T(8,128)}, f32[24,192]{1,0:T(8,128)}, f32[24,192]{1,0:T(8,128)}, f32[8,128]{1,0:T(8,128)}) custom-call(s32[1]{0:T(128)S(6)} %copy.15.count_ref, f32[3]{0:T(128)} %box_ref.3, s32[1]{0:T(128)} %bitcast.lift_ref, f32[48,192]{1,0:T(8,128)} %bitcast.9, f32[48,192]{1,0:T(8,128)} %get-tuple-element.17.near_ref, ...), custom_call_target="tpu_custom_call" | custom-call | tf_op jit(solution)/shard_map/pair_kernel/pallas_call | solution.py:224
  21.6 16.5 %return_kernel.1 = (f32[24,192]{1,0:T(8,128)}, f32[24,192]{1,0:T(8,128)}, f32[4,128]{1,0:T(4,128)}) custom-call(f32[3]{0:T(128)} %box_ref.3, f32[4]{0:T(128)} %extended_ref.1, f32[24,192]{1,0:T(8,128)} %get-tuple-element.21.near_ref, f32[24,192]{1,0:T(8,128)} %get-tuple-element.22.far_ref, f32[8,128]{1,0:T(8,128)} %get-tuple-element.23.sum_ref), custom_call_target="tpu_custom_call" | custom-call | tf_op jit(solution)/shard_map/return_kernel/pallas_call | solution.py:403
  38.1 0.0 copy-start
  38.1 1.2 %slice.10 = f32[1,1]{1,0:T(1,128)} slice(f32[4,128]{1,0:T(4,128)} %get-tuple-element.26.rate_ref), slice={[3:4], [0:1]} | slice | bytes 8 | tf_op jit(solution)/shard_map/slice | solution.py:456
  39.4 0.0 copy-done
  39.4 0.1 slice_reduce_fusion
  39.5 1.2 %pad_maximum_fusion.1 = f32[4]{0:T(128)} fusion(f32[3]{0:T(128)S(1)} %slice_reduce_fusion, f32[1]{0:T(128)} %bitcast.4), kind=kLoop, calls=%fused_computation.2 | loop fusion | flops 4 | bytes 32 | tf_op jit(solution)/shard_map/concatenate | solution.py:456
  40.7 1.6 %final_kernel.1 = (f32[3,1536]{1,0:T(4,128)}, f32[3,1536]{1,0:T(4,128)}, f32[3,1536]{1,0:T(4,128)}) custom-call(f32[24,192]{1,0:T(8,128)} %get-tuple-element.20.own_ref, f32[24,192]{1,0:T(8,128)} %get-tuple-element.24.near_ref, f32[24,192]{1,0:T(8,128)} %get-tuple-element.25.far_ref, f32[4,128]{1,0:T(4,128)} %get-tuple-element.26.rate_ref, ...), custom_call_target="tpu_custom_call" | custom-call | tf_op jit(solution)/shard_map/final_kernel/pallas_call | solution.py:278
Async XLA Ops:
  2.6 0.7 %copy-start.1 = (s32[96]{0:T(128)S(1)}, s32[96]{0:T(128)}, u32[]{:S(2)}) copy-start(s32[96]{0:T(128)} %param.15) | copy-start | bytes 1156
  38.1 1.3 %copy-start = (f32[4,128]{1,0:T(4,128)S(1)}, f32[4,128]{1,0:T(4,128)}, u32[]{:S(2)}) copy-start(f32[4,128]{1,0:T(4,128)} %get-tuple-element.26.rate_ref) | copy-start | bytes 6148
where the time goes:
time: 42.7 us; the launch traced here: 42.3 us
  Pallas kernels  35.3 us (83%)
  local copies, waits for them, and re-layouts  3.72 us (9%)
  other arithmetic  2 us (5%)
  between operations  1.32 us (3%)
    pallas_call x1, Pallas kernels, returned(): pl.pallas_call(functools.partial(return_kernel, count=count, particles=pa...  16.5 us
    pallas_call x1, Pallas kernels, forward(): pl.pallas_call(functools.partial(forward_kernel, count=count), name='forw...  9.72 us
    pallas_call x1, Pallas kernels, pair_forces(): pl.pallas_call(functools.partial(pair_kernel, clusters=clusters, slots=sl...  7.41 us
    pallas_call x1, Pallas kernels, finished(): pl.pallas_call(functools.partial(final_kernel, clusters=clusters), name='...  1.64 us
    slice x2, local copies, waits for them, and re-layouts, on_device(): new_coupling = jnp.concatenate([rates[3:, 0], rates[:3, 0]])  1.36 us
    concatenate x1, other arithmetic, on_device(): new_coupling = jnp.concatenate([rates[3:, 0], rates[:3, 0]])  1.23 us

commit v1 on v0

--- a/solution.py
+++ b/solution.py
@@ -244,7 +244,7 @@
 
 def final_kernel(
     own_ref, near_ref, far_ref, rate_ref, position_ref, velocity_ref, param_ref,
-    force_out, velocity_out, position_out, folded_ref, *, clusters
+    force_out, velocity_out, position_out, coupling_out, folded_ref, *, clusters
 ):
     sublane = lax.broadcasted_iota(jnp.int32, (8, LANES), 0)
     lane = lax.broadcasted_iota(jnp.int32, (8, LANES), 1)
@@ -261,6 +261,10 @@
             force_out[c : c + 1, tile * LANES : (tile + 1) * LANES] = jnp.sum(
                 jnp.where(wanted, picked, 0.0), axis=0, keepdims=True
             )
+    row = jnp.broadcast_to(rate_ref[3:4, :], (1, LANES))
+    for c in range(3):
+        row = jnp.where(lane[0:1] == c + 1, rate_ref[c : c + 1, :], row)
+    coupling_out[...] = row[:, 0:4]
     rates = rate_ref[0:3, 0:1]
     damping = rate_ref[3:4, 0:1]
     velocity = velocity_ref[...]
@@ -278,11 +282,47 @@
     return pl.pallas_call(
         functools.partial(final_kernel, clusters=clusters),
         name="final_kernel",
-        out_shape=(shape,) * 3,
+        out_shape=(shape,) * 3 + (jax.ShapeDtypeStruct((1, 4), jnp.float32),),
         in_specs=[vmem] * 7,
-        out_specs=(vmem,) * 3,
+        out_specs=(vmem,) * 4,
         scratch_shapes=[pltpu.VMEM((24, round_up(clusters, LANES)), jnp.float32)],
     )(own, near_back, far_back, rates, positions, velocities, atom_params)
+
+
+def pack_kernel(position_ref, param_ref, halo_ref, packed_out, chosen_out, *, clusters, far):
+    sublane = lax.broadcasted_iota(jnp.int32, (8, LANES), 0)
+    lane = lax.broadcasted_iota(jnp.int32, (8, LANES), 1)
+    place = (lane & 15) * 8 + sublane
+    for component in range(6):
+        source = position_ref if component < 3 else param_ref
+        row = component % 3
+        for start in range(0, clusters, LANES):
+            width = min(LANES, clusters - start)
+            value = jnp.zeros((8, LANES), jnp.float32)
+            for piece in range(width // 16):
+                at = start * 8 + piece * LANES
+                spread = jnp.broadcast_to(source[row : row + 1, at : at + LANES], (8, LANES))
+                picked = jnp.take_along_axis(spread, place, axis=1, mode="promise_in_bounds")
+                value = jnp.where(lane // 16 == piece, picked, value)
+            packed_out[component * 8 : component * 8 + 8, start : start + width] = value[:, :width]
+    chosen_out[...] = jnp.zeros_like(chosen_out)
+    chosen_out[:, 0:far] = halo_ref[...]
+
+
+def pack(positions, atom_params, halo_far):
+    vmem = pl.BlockSpec(memory_space=pltpu.VMEM)
+    clusters = positions.shape[1] // 8
+    far = halo_far.shape[0]
+    return pl.pallas_call(
+        functools.partial(pack_kernel, clusters=clusters, far=far),
+        name="pack_kernel",
+        out_shape=(
+            jax.ShapeDtypeStruct((48, clusters), jnp.float32),
+            jax.ShapeDtypeStruct((1, round_up(far, LANES)), jnp.int32),
+        ),
+        in_specs=[vmem] * 3,
+        out_specs=(vmem,) * 2,
+    )(positions, atom_params, halo_far[None, :])
 
 
 def send(source, target, sems, place, device):
@@ -437,9 +477,7 @@
     far_clusters = halo_far.shape[0]
     slots = 2 * clusters + far_clusters
     axis_count = lax.axis_size("gx")
-    packed = jnp.concatenate([positions, atom_params[:3]], axis=0)
-    packed = packed.reshape(6, clusters, 8).transpose(0, 2, 1).reshape(48, clusters)
-    chosen = jnp.pad(halo_far, (0, round_up(far_clusters, LANES) - far_clusters))[None, :]
+    packed, chosen = pack(positions, atom_params, halo_far)
     near_rows, beyond, picked = forward(packed, chosen, axis_count)
     lift = (lax.axis_index("gx") - (axis_count - 2)).astype(jnp.int32)[None]
     own, near, far, sums = pair_forces(
@@ -450,11 +488,10 @@
     near_back, far_back, rates = returned(
         box_lengths, extended_variables, near, far, sums, axis_count, atoms_here * axis_count
     )
-    forces, new_velocities, new_positions = finished(
+    forces, new_velocities, new_positions, new_coupling = finished(
         own, near_back, far_back, rates, positions, velocities, atom_params
     )
-    new_coupling = jnp.concatenate([rates[3:, 0], rates[:3, 0]])
-    return (forces, new_velocities, new_positions, new_coupling)
+    return (forces, new_velocities, new_positions, new_coupling.reshape(4))
 
 
 def solution(mesh):

time: 42.7 us -> 38.5 us (0.902)
  local copies, waits for them, and re-layouts: 3.72 us -> 0 us
  other arithmetic: 2 us -> 0 us
  Pallas kernels: 35.3 us -> 36.6 us
    concatenate x2 -> x0, other arithmetic: 2 us -> none  [the longest x1 1.23 us: on_device(): new_coupling = jnp.concatenate([rates[3:, 0], rates[:3, 0]])]
    pallas_call x0 -> x1, Pallas kernels: none -> 1.52 us  [pack(): pl.pallas_call(functools.partial(pack_kernel, clusters=clusters, far=far)...]
    slice x2 -> x0, local copies, waits for them, and re-layouts: 1.36 us -> none  [on_device(): new_coupling = jnp.concatenate([rates[3:, 0], rates[:3, 0]])]
    transpose x1 -> x0, local copies, waits for them, and re-layouts: 0.85 us -> none  [on_device(): packed.reshape(6, clusters, 8).transpose(0, 2, 1).reshape(48, clusters)]
    unnamed x4 -> x0, local copies, waits for them, and re-layouts: 0.66 us -> none
    broadcast_in_dim x1 -> x0, local copies, waits for them, and re-layouts: 0.51 us -> none  [on_device(): jnp.pad(halo_far, (0, round_up(far_clusters, LANES) - far_clusters))]
where the time goes in v1:
time: 38.5 us; the launch traced here: 37.9 us
  Pallas kernels  36.6 us (95%)
  between operations  1.3 us (3%)
    pallas_call x1, Pallas kernels, returned(): pl.pallas_call(functools.partial(return_kernel, count=count, particles=pa...  16.7 us
    pallas_call x1, Pallas kernels, forward(): pl.pallas_call(functools.partial(forward_kernel, count=count), name='forw...  9.71 us
    pallas_call x1, Pallas kernels, pair_forces(): pl.pallas_call(functools.partial(pair_kernel, clusters=clusters, slots=sl...  7.03 us
    pallas_call x1, Pallas kernels, finished(): pl.pallas_call(functools.partial(final_kernel, clusters=clusters), name='...  1.65 us
    pallas_call x1, Pallas kernels, pack(): pl.pallas_call(functools.partial(pack_kernel, clusters=clusters, far=far)...  1.52 us

profile of v1, /device:TPU:0, one launch (start us, length us, event | category | flops | bytes accessed | tf_op | source)
XLA Modules:
  0.0 37.9 jit_solution(9343904956236222319)
XLA Ops:
  1.3 1.5 %pack_kernel.1 = (f32[48,192]{1,0:T(8,128)}, s32[1,128]{1,0:T(1,128)}) custom-call(f32[3,1536]{1,0:T(4,128)} %position_ref.3, f32[4,1536]{1,0:T(4,128)} %param_ref.5, s32[1,96]{1,0:T(1,128)} %bitcast.3), custom_call_target="tpu_custom_call" | custom-call | tf_op jit(solution)/shard_map/pack_kernel/pallas_call | solution.py:316
  2.8 9.7 %forward_kernel.1 = (f32[48,192]{1,0:T(8,128)}, f32[48,192]{1,0:T(8,128)}, s32[1,128]{1,0:T(1,128)}) custom-call(f32[48,192]{1,0:T(8,128)} %get-tuple-element.20.packed_ref.here_ref, s32[1,128]{1,0:T(1,128)} %get-tuple-element.21.chosen_ref), custom_call_target="tpu_custom_call" | custom-call | tf_op jit(solution)/shard_map/forward_kernel/pallas_call | solution.py:364
  12.5 7.0 %pair_kernel.1 = (f32[24,192]{1,0:T(8,128)}, f32[24,192]{1,0:T(8,128)}, f32[24,192]{1,0:T(8,128)}, f32[8,128]{1,0:T(8,128)}) custom-call(s32[1]{0:T(128)S(6)} %copy.13.count_ref, f32[3]{0:T(128)} %box_ref.3, s32[1]{0:T(128)} %bitcast.lift_ref, f32[48,192]{1,0:T(8,128)} %get-tuple-element.20.packed_ref.here_ref, f32[48,192]{1,0:T(8,128)} %get-tuple-element.22.near_ref, ...), custom_call_target="tpu_custom_call" | custom-call | tf_op jit(solution)/shard_map/pair_kernel/pallas_call | solution.py:224
  19.6 16.7 %return_kernel.1 = (f32[24,192]{1,0:T(8,128)}, f32[24,192]{1,0:T(8,128)}, f32[4,128]{1,0:T(4,128)}) custom-call(f32[3]{0:T(128)} %box_ref.3, f32[4]{0:T(128)} %extended_ref.1, f32[24,192]{1,0:T(8,128)} %get-tuple-element.26.near_ref, f32[24,192]{1,0:T(8,128)} %get-tuple-element.27.far_ref, f32[8,128]{1,0:T(8,128)} %get-tuple-element.28.sum_ref), custom_call_target="tpu_custom_call" | custom-call | tf_op jit(solution)/shard_map/return_kernel/pallas_call | solution.py:443
  36.2 1.6 %final_kernel.1 = (f32[3,1536]{1,0:T(4,128)}, f32[3,1536]{1,0:T(4,128)}, f32[3,1536]{1,0:T(4,128)}, f32[1,4]{1,0:T(1,128)}) custom-call(f32[24,192]{1,0:T(8,128)} %get-tuple-element.25.own_ref, f32[24,192]{1,0:T(8,128)} %get-tuple-element.29.near_ref, f32[24,192]{1,0:T(8,128)} %get-tuple-element.30.far_ref, f32[4,128]{1,0:T(4,128)} %get-tuple-element.31.rate_ref, ...), custom_call_target="tpu_custom_call" | custom-call | tf_op jit(solution)/shard_map/final_kernel/pallas_call | solution.py:282
